TPU v7x, 32 devices: a whole 2x2x4 slice. The times are simulated.
32 devices in a mesh: obs: 2 (over y), bt: 4 (over z), freq: 2 (over x), pol: 2 (over core).
Axes of the slice: x: 2, y: 2, z: 4, core: 2. Of those that a mesh axis runs over, the one named last changes fastest.
Arguments:
- gains: float32 [16, 4, 8, 1984], P(('obs', 'bt', 'pol'), 'freq'), parts along dimension 0, may hold values from -3 to 3
- visibilities: bfloat16 [16, 4, 8, 4096], P('obs', 'freq', None, ('bt', 'pol')), parts along dimension 0, may hold values from -6 to 6
- first_station: int32 [8192], P(('obs', 'bt', 'pol')), parts along dimension 0, may hold values from 0 to 61
- second_station: int32 [8192], P(('obs', 'bt', 'pol')), parts along dimension 0, may hold values from 0 to 61, as said below
- filled_row_count: int32 [16], P(('obs', 'bt', 'pol')), parts along dimension 0, may hold values from 256 to 512
- facet_dir: int32 [16], P('obs'), parts along dimension 0, may hold values from 0 to 7, each once
Outputs:
- corrected: bfloat16 [16, 4, 8, 4096], P('obs', 'freq', None, ('bt', 'pol')), parts along dimension 0
There are 2 independent parts, one for each index of `obs`. A program takes and returns all parts, laid end to end along the dimension named above; each array names one. Nothing has to cross between parts.
Inputs may be any that keep to these rules, and one draw needn't show every extreme that they name: In every row second_station differs from first_station. `facet_dir`: each direction names exactly one facet.
All inputs are finite; a program needn't handle non-finite values.
Results may differ from a plain program's by a relative error of at most 0.001.
Values sent between devices are 32-bit elements; how exact they have to be, the bound alone decides.
No kernel may reach another device: no remote copies, remote signals or barrier semaphores. Data moves between devices by JAX's collectives and lax.ppermute only.
A program may use at most 64 MiB of HBM per device.

v0:
```python
import jax
import jax.numpy as jnp
from jax import lax
from jax.sharding import PartitionSpec as P

ARRAY_STATIONS = 62
GAIN_SLOT_COUNT = 4


def entry(values, row_at, col_at):
    return (values[..., 2 * row_at + col_at, :], values[..., 4 + 2 * row_at + col_at, :])


def apply_jones(left_matrix, data, right_matrix):
    real_parts = []
    imag_parts = []
    for out_row in (0, 1):
        for out_col in (0, 1):
            total_re = jnp.zeros_like(left_matrix[..., 0, :])
            total_im = jnp.zeros_like(left_matrix[..., 0, :])
            for middle in (0, 1):
                for column in (0, 1):
                    left_re, left_im = entry(left_matrix, out_row, middle)
                    data_re, data_im = entry(data, middle, column)
                    right_re, right_im = entry(right_matrix, out_col, column)
                    prod_re = left_re * data_re - left_im * data_im
                    prod_im = left_re * data_im + left_im * data_re
                    total_re = total_re + prod_re * right_re + prod_im * right_im
                    total_im = total_im + prod_im * right_re - prod_re * right_im
            real_parts.append(total_re)
            imag_parts.append(total_im)
    return jnp.stack(real_parts + imag_parts, axis=-2)


def expand_slots(gain_window, antenna, block_rows, slots, stations):
    facets, chans, comps, _ = gain_window.shape
    current = gain_window[..., : slots * stations].reshape(facets, chans, comps, slots, stations)
    following = gain_window[..., stations:].reshape(facets, chans, comps, slots, stations)
    paired = jnp.concatenate([current, following], axis=4)
    per_slot = block_rows // slots
    grouped = antenna.reshape(slots, per_slot)
    fraction = (jnp.arange(per_slot, dtype=jnp.int32).astype(jnp.float32) + 0.5) / per_slot
    station_ids = jnp.arange(stations, dtype=jnp.int32)
    station_mask = (station_ids[None, :, None] == grouped[:, None, :]).astype(jnp.float32)
    table = jnp.concatenate([station_mask * (1.0 - fraction), station_mask * fraction], axis=1)
    spread = jnp.einsum("fckjn,jnp->fckjp", paired, table, precision=lax.Precision.HIGHEST)
    return spread.reshape(facets, chans, comps, block_rows)


def apply_correction(
    gain_window, block_visibilities, first_station_gain, second_station_gain, filled_rows
):
    block_rows = block_visibilities.shape[3]
    left_matrix = expand_slots(
        gain_window, first_station_gain, block_rows, GAIN_SLOT_COUNT, ARRAY_STATIONS
    )
    right_matrix = expand_slots(
        gain_window, second_station_gain, block_rows, GAIN_SLOT_COUNT, ARRAY_STATIONS
    )
    product = apply_jones(left_matrix, block_visibilities.astype(jnp.float32), right_matrix)
    live_mask = jnp.arange(block_rows, dtype=jnp.int32) < filled_rows
    return jnp.where(live_mask, product, 0.0 * product).astype(jnp.bfloat16)


def relay(payload):
    relaid = lax.all_to_all(payload, ("bt", "pol"), split_axis=3, concat_axis=0, tiled=True)
    return relaid


def select_facets(relaid, facet_dir):
    directions = relaid.shape[0]
    onehot = (facet_dir[:, None] == jnp.arange(directions, dtype=jnp.int32)[None, :]).astype(
        jnp.float32
    )
    return jnp.einsum("fd,dckn->fckn", onehot, relaid, precision=lax.Precision.HIGHEST)


def shards(gains, visibilities, first_station, second_station, filled_row_count, facet_dir):
    block_count = lax.axis_size(("bt", "pol"))
    dirs_here, chans_here, comps, _ = gains.shape
    by_slot = gains.reshape(
        dirs_here, chans_here, comps, block_count, GAIN_SLOT_COUNT, ARRAY_STATIONS
    )
    firsts = by_slot[:, :, :, :, 0, :]
    final_one = by_slot[:, :, :, block_count - 1 :, GAIN_SLOT_COUNT - 1, :]
    nexts = jnp.concatenate([firsts[:, :, :, 1:, :], final_one], axis=3)
    own_slots = by_slot.reshape(
        dirs_here, chans_here, comps, block_count, GAIN_SLOT_COUNT * ARRAY_STATIONS
    )
    windows = jnp.concatenate([own_slots, nexts], axis=4)
    windows = windows.reshape(
        dirs_here, chans_here, comps, block_count * (GAIN_SLOT_COUNT + 1) * ARRAY_STATIONS
    )
    gain_window = select_facets(relay(windows), facet_dir)
    return apply_correction(
        gain_window, visibilities, first_station, second_station, filled_row_count[0]
    )


def solution(mesh):
    return jax.shard_map(
        shards,
        mesh=mesh,
        in_specs=(
            P(("obs", "bt", "pol"), "freq", None, None),
            P("obs", "freq", None, ("bt", "pol")),
            P(("obs", "bt", "pol")),
            P(("obs", "bt", "pol")),
            P(("obs", "bt", "pol")),
            P("obs"),
        ),
        out_specs=P("obs", "freq", None, ("bt", "pol")),
        check_vma=False,
    )
```

profile of v0, /device:TPU:0, one launch (start us, length us, event | category | flops | bytes accessed | tf_op | source)
XLA Modules:
  0.0 31.5 jit_solution(10585168810742284929)
XLA Ops:
  0.0 1.3 %reshape.32 = f32[1,2,8,8,4,62]{5,4,3,2,1,0:T(4,128)S(1)} reshape(f32[1,2,8,1984]{3,2,1,0:T(8,128)} %param.6) | data formatting | bytes 253952 | tf_op jit(solution)/shard_map/reshape | solution.py:81
  1.4 1.0 %reshape_reshape.3 = f32[1,2,8,8,248]{4,3,2,1,0:T(8,128)S(1)} reshape(f32[1,2,8,1984]{3,2,1,0:T(8,128)} %param.6) | data formatting | bytes 253952 | tf_op jit(solution)/shard_map/reshape;reshape | solution.py:87
  2.4 0.1 maximum_maximum_fusion
  2.6 2.2 %copy.38 = f32[1,2,8,8,310]{2,1,4,3,0:T(2,128)S(1)} copy(f32[1,2,8,8,310]{4,3,2,1,0:T(8,128)S(1)} %maximum_maximum_fusion) | data formatting | bytes 317440 | tf_op jit(solution)/shard_map/concatenate | solution.py:90
  4.8 4.0 %reshape.41 = f32[8,1,4960]{2,1,0:T(1,128)} reshape(f32[2480,1,2,8]{3,2,1,0:T(2,128)S(1)} %bitcast.55) | data formatting | bytes 317440
  8.8 6.4 %all-to-all-start = ((f32[8,1,4960]{2,1,0:T(1,128)}), f32[8,1,4960]{2,1,0:T(1,128)S(1)}, u32[]{:S(2)}, u32[]{:S(2)}) async-start(f32[8,1,4960]{2,1,0:T(1,128)} %reshape.41), calls=%async_computation | async-start | bytes 319488 | tf_op jit(solution)/shard_map/all_to_all | solution.py:66
  16.0 6.3 %all-to-all-done = f32[8,1,4960]{2,1,0:T(1,128)S(1)} async-done(((f32[8,1,4960]{2,1,0:T(1,128)}), f32[8,1,4960]{2,1,0:T(1,128)S(1)}, u32[]{:S(2)}, u32[]{:S(2)}) %all-to-all-start) | async-done | bytes 158752 | tf_op jit(solution)/shard_map/all_to_all | solution.py:66
  22.3 0.5 %broadcast.50 = f32[]{:T(128)} broadcast(f32[]{:T(128)} %constant.71), dimensions={} | broadcast | bytes 8 | tf_op jit(solution)/shard_map/all_to_all | solution.py:66
  22.8 1.0 %reduce = f32[8,4960]{1,0:T(8,128)S(1)} reduce(f32[8,1,4960]{2,1,0:T(1,128)S(1)} %all-to-all-done, f32[]{:T(128)} %broadcast.50), dimensions={1}, to_apply=%all_to_all.13.reduce_sub_computation | reduce | bytes 317444 | tf_op jit(solution)/shard_map/all_to_all | solution.py:66
  23.8 2.0 %reshape.42 = f32[2480,1,2,8]{3,2,1,0:T(2,128)S(1)} reshape(f32[8,4960]{1,0:T(8,128)S(1)} %reduce) | data formatting | bytes 317440
  25.8 2.1 %copy.65 = f32[1,2,8,8,310]{4,3,2,1,0:T(8,128)S(1)} copy(f32[1,2,8,8,310]{2,1,4,3,0:T(2,128)S(1)} %bitcast.56) | data formatting | bytes 317440 | tf_op jit(solution)/shard_map/all_to_all | solution.py:66
  27.9 0.3 fusion.5
  28.2 0.1 fusion.18
  28.3 0.2 reshape.34
  28.5 0.2 copy.40
  28.6 0.2 reshape.35
  28.8 0.2 copy.41
  29.0 0.4 %convolution_bitcast_fusion = f32[8,2,8,4,128]{4,2,1,0,3:T(8,128)S(1)} fusion(f32[4,62,128]{2,1,0:T(8,128)S(1)} %get-tuple-element.44, f32[4,62,128]{2,1,0:T(8,128)S(1)} %get-tuple-element.43, f32[8,2,8,4,62]{4,2,1,0,3:T(8,128)S(1)} %copy.41, f32[8,2,8,4,62]{4,2,1,0,3:T(8,128)S(1)} %copy.40), kind=kOutput, calls=%fused_computation | convolution fusion | flops 97644544 | bytes 770048 | tf_op jit(solution)/shard_map/fckjn,jnp->fckjp/dot_general | solution.py:46
  29.5 0.2 fusion.17
  29.6 0.4 %convolution_bitcast_fusion.1 = f32[8,2,8,4,128]{4,2,1,0,3:T(8,128)S(1)} fusion(f32[4,62,128]{2,1,0:T(8,128)S(1)} %get-tuple-element.45, f32[4,62,128]{2,1,0:T(8,128)S(1)} %get-tuple-element.46, f32[8,2,8,4,62]{4,2,1,0,3:T(8,128)S(1)} %copy.41, f32[8,2,8,4,62]{4,2,1,0,3:T(8,128)S(1)} %copy.40), kind=kOutput, calls=%fused_computation.1 | convolution fusion | flops 97644544 | bytes 770048 | tf_op jit(solution)/shard_map/fckjn,jnp->fckjp/dot_general | solution.py:46
  30.1 0.2 fusion.16
  30.3 0.1 add_dynamic-update-slice_fusion.3
  30.4 0.1 add_dynamic-update-slice_fusion.1
  30.8 0.7 %copy.61 = bf16[8,2,8,512]{3,2,1,0:T(8,128)(2,1)} copy(bf16[8,2,8,512]{3,0,2,1:T(8,128)(2,1)S(1)} %fusion) | data formatting | bytes 262144 | tf_op jit(solution)/shard_map/convert_element_type | solution.py:62
  (24 shorter events, 0.6 us)
Async XLA Ops:
  2.6 12.6 %copy-start = (bf16[8,2,8,512]{3,2,1,0:T(8,128)(2,1)S(1)}, bf16[8,2,8,512]{3,2,1,0:T(8,128)(2,1)}, u32[]{:S(2)}) copy-start(bf16[8,2,8,512]{3,2,1,0:T(8,128)(2,1)} %param.7) | copy-start | bytes 393220
  2.6 13.3 %copy-start.1 = (s32[512]{0:T(512)S(1)}, s32[512]{0:T(512)}, u32[]{:S(2)}) copy-start(s32[512]{0:T(512)} %param.9) | copy-start | bytes 6148
  2.6 13.3 %copy-start.2 = (s32[512]{0:T(512)S(1)}, s32[512]{0:T(512)}, u32[]{:S(2)}) copy-start(s32[512]{0:T(512)} %param.8) | copy-start | bytes 6148
  8.8 13.5 %all-to-all-start = ((f32[8,1,4960]{2,1,0:T(1,128)}), f32[8,1,4960]{2,1,0:T(1,128)S(1)}, u32[]{:S(2)}, u32[]{:S(2)}) async-start(f32[8,1,4960]{2,1,0:T(1,128)} %reshape.41), calls=%async_computation | async-start | bytes 319488 | tf_op jit(solution)/shard_map/all_to_all | solution.py:66
  23.8 4.1 %copy-start.3 = (s32[8]{0:T(128)S(1)}, s32[8]{0:T(128)}, u32[]{:S(2)}) copy-start(s32[8]{0:T(128)} %param.11) | copy-start | bytes 100
where the time goes:
time: 31.8 us; the launch traced here: 31.5 us
  local copies, waits for them, and re-layouts  15 us (47%)
  starting transfers between devices  6.35 us (20%)
  waiting for transfers between devices  6.29 us (20%)
  other arithmetic  1.77 us (6%)
  matrix products  1.16 us (4%)
  between operations  0.94 us (3%)
    all_to_all x1, starting transfers between devices, relay(): lax.all_to_all(payload, ('bt', 'pol'), split_axis=3, concat_axis=0, tiled...  6.35 us
    all_to_all x1, waiting for transfers between devices, relay(): lax.all_to_all(payload, ('bt', 'pol'), split_axis=3, concat_axis=0, tiled...  6.29 us
    unnamed x10, local copies, waits for them, and re-layouts  5.99 us
    all_to_all x2, local copies, waits for them, and re-layouts, relay(): lax.all_to_all(payload, ('bt', 'pol'), split_axis=3, concat_axis=0, tiled...  2.57 us
    concatenate x1, local copies, waits for them, and re-layouts, shards(): windows = jnp.concatenate([own_slots, nexts], axis=4)  2.18 us
    reshape x1, local copies, waits for them, and re-layouts, shards(): gains.reshape(dirs_here, chans_here, comps, block_count, GAIN_SLOT_COUNT,...  1.31 us
    another operation x1, local copies, waits for them, and re-layouts, shards(): by_slot.reshape(dirs_here, chans_here, comps, block_count, GAIN_SLOT_COUN...  1.03 us
    all_to_all x1, other arithmetic, relay(): lax.all_to_all(payload, ('bt', 'pol'), split_axis=3, concat_axis=0, tiled...  1.02 us
  transfers between devices with their start and end apart: 1, of which 1 were waited for; matrix products, arithmetic and copies ran while one was open for 0% of the time, Pallas kernels for 0%

commit v1 on v0

--- a/solution.py
+++ b/solution.py
@@ -63,7 +63,12 @@
 
 
 def relay(payload):
-    relaid = lax.all_to_all(payload, ("bt", "pol"), split_axis=3, concat_axis=0, tiled=True)
+    relaid = jnp.concatenate(
+        lax.all_to_all(
+            jnp.stack(jnp.split(payload, lax.axis_size(("bt", "pol")), axis=3)), ("bt", "pol"), 0, 0
+        ),
+        axis=0,
+    )
     return relaid
 
 

time: 31.8 us -> 26.7 us (0.84)
  local copies, waits for them, and re-layouts: 15 us -> 10.4 us
  other arithmetic: 1.77 us -> 0.75 us
  waiting for transfers between devices: 6.29 us -> 6.79 us
    all_to_all x2 -> x0, local copies, waits for them, and re-layouts: 2.57 us -> none  [relay(): lax.all_to_all(payload, ('bt', 'pol'), split_axis=3, concat_axis=0, tiled...]
    concatenate x1 -> x0, local copies, waits for them, and re-layouts: 2.18 us -> none  [shards(): windows = jnp.concatenate([own_slots, nexts], axis=4)]
    all_to_all x1 -> x0, other arithmetic: 1.02 us -> none  [relay(): lax.all_to_all(payload, ('bt', 'pol'), split_axis=3, concat_axis=0, tiled...]
    another operation x1, local copies, waits for them, and re-layouts: 1.03 us -> 0.12 us  [shards(): by_slot.reshape(dirs_here, chans_here, comps, block_count, GAIN_SLOT_COUN...]
    another operation x0 -> x1, local copies, waits for them, and re-layouts: none -> 0.67 us  [relay(): jnp.stack(jnp.split(payload, lax.axis_size(('bt', 'pol')), axis=3))]
    all_to_all x1, waiting for transfers between devices: 6.29 us -> 6.79 us  [relay(): lax.all_to_all(jnp.stack(jnp.split(payload, lax.axis_size(('bt', 'pol')),...]
    unnamed x10 -> x17, local copies, waits for them, and re-layouts: 5.99 us -> 6.21 us
  transfers between devices with their start and end apart: 1 -> 1, of which waited for: 1 -> 1; matrix products, arithmetic and copies ran while one was open for 0% -> 1% of each run, Pallas kernels for 0% -> 0%
where the time goes in v1:
time: 26.7 us; the launch traced here: 26.4 us
  local copies, waits for them, and re-layouts  10.4 us (39%)
  waiting for transfers between devices  6.79 us (25%)
  starting transfers between devices  6.49 us (24%)
  matrix products  1.15 us (4%)
  between operations  0.9 us (3%)
  other arithmetic  0.75 us (3%)
    all_to_all x1, waiting for transfers between devices, relay(): lax.all_to_all(jnp.stack(jnp.split(payload, lax.axis_size(('bt', 'pol')),...  6.79 us
    all_to_all x1, starting transfers between devices, relay(): lax.all_to_all(jnp.stack(jnp.split(payload, lax.axis_size(('bt', 'pol')),...  6.49 us
    unnamed x17, local copies, waits for them, and re-layouts  6.21 us
    reshape x1, local copies, waits for them, and re-layouts, shards(): gains.reshape(dirs_here, chans_here, comps, block_count, GAIN_SLOT_COUNT,...  1.31 us
    dot_general x2, matrix products, expand_slots(): jnp.einsum('fckjn,jnp->fckjp', paired, table, precision=lax.Precision.HIG...  0.87 us
    convert_element_type x1, local copies, waits for them, and re-layouts, apply_correction(): return jnp.where(live_mask, product, 0.0 * product).astype(jnp.bfloat16)  0.7 us
    another operation x1, local copies, waits for them, and re-layouts, relay(): jnp.stack(jnp.split(payload, lax.axis_size(('bt', 'pol')), axis=3))  0.67 us
  transfers between devices with their start and end apart: 1, of which 1 were waited for; matrix products, arithmetic and copies ran while one was open for 1% of the time, Pallas kernels for 0%

profile of v1, /device:TPU:0, one launch (start us, length us, event | category | flops | bytes accessed | tf_op | source)
XLA Modules:
  0.0 26.4 jit_solution(16037608046344883767)
XLA Ops:
  0.0 1.3 %reshape.35 = f32[1,2,8,8,4,62]{5,4,3,2,1,0:T(4,128)S(1)} reshape(f32[1,2,8,1984]{3,2,1,0:T(8,128)} %param.6) | data formatting | bytes 253952 | tf_op jit(solution)/shard_map/reshape | solution.py:86
  1.4 0.8 %copy-done = f32[1,2,8,1984]{3,2,1,0:T(8,128)S(1)} copy-done((f32[1,2,8,1984]{3,2,1,0:T(8,128)S(1)}, f32[1,2,8,1984]{3,2,1,0:T(8,128)}, u32[]{:S(2)}) %copy-start) | copy-done | bytes 127000
  2.4 0.1 maximum_maximum_fusion
  2.6 0.6 %constant_dynamic-update-slice_fusion.7 = f32[8,1,2,8,310]{4,3,2,1,0:T(8,128)} fusion(f32[1,2,8,2480]{3,2,1,0:T(8,128)S(1)} %reshape.36), kind=kLoop, calls=%fused_computation.31 | loop fusion | bytes 44416
  3.2 0.7 %constant_dynamic-update-slice_fusion.6 = f32[8,1,2,8,310]{4,3,2,1,0:T(8,128)} fusion(f32[8,1,2,8,310]{4,3,2,1,0:T(8,128)} %constant_dynamic-update-slice_fusion.7, f32[1,2,8,2480]{3,2,1,0:T(8,128)S(1)} %reshape.36), kind=kLoop, calls=%fused_computation.30 | loop fusion | bytes 44416
  3.9 0.7 %constant_dynamic-update-slice_fusion.5 = f32[8,1,2,8,310]{4,3,2,1,0:T(8,128)} fusion(f32[8,1,2,8,310]{4,3,2,1,0:T(8,128)} %constant_dynamic-update-slice_fusion.6, f32[1,2,8,2480]{3,2,1,0:T(8,128)S(1)} %reshape.36), kind=kLoop, calls=%fused_computation.29 | loop fusion | bytes 44416
  4.6 0.7 %constant_dynamic-update-slice_fusion.4 = f32[8,1,2,8,310]{4,3,2,1,0:T(8,128)} fusion(f32[8,1,2,8,310]{4,3,2,1,0:T(8,128)} %constant_dynamic-update-slice_fusion.5, f32[1,2,8,2480]{3,2,1,0:T(8,128)S(1)} %reshape.36), kind=kLoop, calls=%fused_computation.28 | loop fusion | bytes 44416
  5.3 0.7 %constant_dynamic-update-slice_fusion.3 = f32[8,1,2,8,310]{4,3,2,1,0:T(8,128)} fusion(f32[8,1,2,8,310]{4,3,2,1,0:T(8,128)} %constant_dynamic-update-slice_fusion.4, f32[1,2,8,2480]{3,2,1,0:T(8,128)S(1)} %reshape.36), kind=kLoop, calls=%fused_computation.27 | loop fusion | bytes 44416
  6.0 0.7 %constant_dynamic-update-slice_fusion.2 = f32[8,1,2,8,310]{4,3,2,1,0:T(8,128)} fusion(f32[8,1,2,8,310]{4,3,2,1,0:T(8,128)} %constant_dynamic-update-slice_fusion.3, f32[1,2,8,2480]{3,2,1,0:T(8,128)S(1)} %reshape.36), kind=kLoop, calls=%fused_computation.26 | loop fusion | bytes 44416
  6.7 0.7 %constant_dynamic-update-slice_fusion.1 = f32[8,1,2,8,310]{4,3,2,1,0:T(8,128)} fusion(f32[8,1,2,8,310]{4,3,2,1,0:T(8,128)} %constant_dynamic-update-slice_fusion.2, f32[1,2,8,2480]{3,2,1,0:T(8,128)S(1)} %reshape.36), kind=kLoop, calls=%fused_computation.25 | loop fusion | bytes 44416
  7.3 0.7 %constant_dynamic-update-slice_fusion = f32[8,1,2,8,310]{4,3,2,1,0:T(8,128)} fusion(f32[8,1,2,8,310]{4,3,2,1,0:T(8,128)} %constant_dynamic-update-slice_fusion.1, f32[1,2,8,2480]{3,2,1,0:T(8,128)S(1)} %reshape.36), kind=kLoop, calls=%fused_computation.24 | loop fusion | bytes 44416 | tf_op jit(solution)/shard_map/stack | solution.py:68
  8.0 6.5 %all-to-all-start = ((f32[8,1,2,8,310]{4,3,2,1,0:T(8,128)}), f32[8,1,2,8,310]{4,3,2,1,0:T(8,128)S(1)}, u32[]{:S(2)}, u32[]{:S(2)}) async-start(f32[8,1,2,8,310]{4,3,2,1,0:T(8,128)} %constant_dynamic-update-slice_fusion), calls=%async_computation | async-start | bytes 393216 | tf_op jit(solution)/shard_map/all_to_all | solution.py:67
  15.3 0.7 %copy-done.3 = s32[512]{0:T(512)S(1)} copy-done((s32[512]{0:T(512)S(1)}, s32[512]{0:T(512)}, u32[]{:S(2)}) %copy-start.3) | copy-done | bytes 2072
  16.0 6.8 %all-to-all-done = f32[8,1,2,8,310]{4,3,2,1,0:T(8,128)S(1)} async-done(((f32[8,1,2,8,310]{4,3,2,1,0:T(8,128)}), f32[8,1,2,8,310]{4,3,2,1,0:T(8,128)S(1)}, u32[]{:S(2)}, u32[]{:S(2)}) %all-to-all-start) | async-done | bytes 158752 | tf_op jit(solution)/shard_map/all_to_all | solution.py:67
  22.8 0.3 %fusion.5 = f32[8,2,8,310]{3,0,2,1:T(8,128)S(1)} fusion(f32[8,1,2,8,310]{4,3,2,1,0:T(8,128)S(1)} %all-to-all-done, s32[8]{0:T(128)S(1)} %copy-done.4), kind=kOutput, calls=%fused_computation.14 | convolution fusion | flops 3809344 | bytes 317472 | tf_op jit(solution)/shard_map/fd,dckn->fckn/dot_general | solution.py:80
  23.2 0.2 reshape.38
  23.4 0.2 copy.27
  23.5 0.2 reshape.39
  23.7 0.2 copy.28
  23.9 0.4 %convolution_bitcast_fusion.1 = f32[8,2,8,4,128]{4,2,1,0,3:T(8,128)S(1)} fusion(f32[4,62,128]{2,1,0:T(8,128)S(1)} %get-tuple-element.45, f32[4,62,128]{2,1,0:T(8,128)S(1)} %get-tuple-element.46, f32[8,2,8,4,62]{4,2,1,0,3:T(8,128)S(1)} %copy.28, f32[8,2,8,4,62]{4,2,1,0,3:T(8,128)S(1)} %copy.27), kind=kOutput, calls=%fused_computation.1 | convolution fusion | flops 97644544 | bytes 770048 | tf_op jit(solution)/shard_map/fckjn,jnp->fckjp/dot_general | solution.py:46
  24.4 0.2 fusion.17
  24.5 0.4 %convolution_bitcast_fusion = f32[8,2,8,4,128]{4,2,1,0,3:T(8,128)S(1)} fusion(f32[4,62,128]{2,1,0:T(8,128)S(1)} %get-tuple-element.44, f32[4,62,128]{2,1,0:T(8,128)S(1)} %get-tuple-element.43, f32[8,2,8,4,62]{4,2,1,0,3:T(8,128)S(1)} %copy.28, f32[8,2,8,4,62]{4,2,1,0,3:T(8,128)S(1)} %copy.27), kind=kOutput, calls=%fused_computation | convolution fusion | flops 97644544 | bytes 770048 | tf_op jit(solution)/shard_map/fckjn,jnp->fckjp/dot_general | solution.py:46
  25.0 0.2 fusion.18
  25.7 0.7 %copy.48 = bf16[8,2,8,512]{3,2,1,0:T(8,128)(2,1)} copy(bf16[8,2,8,512]{3,0,2,1:T(8,128)(2,1)S(1)} %fusion) | data formatting | bytes 262144 | tf_op jit(solution)/shard_map/convert_element_type | solution.py:62
  (29 shorter events, 1.1 us)
Async XLA Ops:
  1.3 0.9 %copy-start = (f32[1,2,8,1984]{3,2,1,0:T(8,128)S(1)}, f32[1,2,8,1984]{3,2,1,0:T(8,128)}, u32[]{:S(2)}) copy-start(f32[1,2,8,1984]{3,2,1,0:T(8,128)} %param.6) | copy-start | bytes 380932
  8.0 6.5 %copy-start.1 = (bf16[8,2,8,512]{3,2,1,0:T(8,128)(2,1)S(1)}, bf16[8,2,8,512]{3,2,1,0:T(8,128)(2,1)}, u32[]{:S(2)}) copy-start(bf16[8,2,8,512]{3,2,1,0:T(8,128)(2,1)} %param.7) | copy-start | bytes 393220
  8.0 14.8 %all-to-all-start = ((f32[8,1,2,8,310]{4,3,2,1,0:T(8,128)}), f32[8,1,2,8,310]{4,3,2,1,0:T(8,128)S(1)}, u32[]{:S(2)}, u32[]{:S(2)}) async-start(f32[8,1,2,8,310]{4,3,2,1,0:T(8,128)} %constant_dynamic-update-slice_fusion), calls=%async_computation | async-start | bytes 393216 | tf_op jit(solution)/shard_map/all_to_all | solution.py:67
  15.3 0.7 %copy-start.3 = (s32[512]{0:T(512)S(1)}, s32[512]{0:T(512)}, u32[]{:S(2)}) copy-start(s32[512]{0:T(512)} %param.8) | copy-start | bytes 6148
  15.3 0.7 %copy-start.2 = (s32[512]{0:T(512)S(1)}, s32[512]{0:T(512)}, u32[]{:S(2)}) copy-start(s32[512]{0:T(512)} %param.9) | copy-start | bytes 6148
  16.0 6.8 %copy-start.4 = (s32[8]{0:T(128)S(1)}, s32[8]{0:T(128)}, u32[]{:S(2)}) copy-start(s32[8]{0:T(128)} %param.11) | copy-start | bytes 100
